TPU v7x, 256 devices: a whole 4x4x8 slice. The times are simulated.
256 devices in a mesh: pole: 4 (over y), tile: 64 (over z, x, core).
Axes of the slice: x: 4, y: 4, z: 8, core: 2. Of those that a mesh axis runs over, the one named last changes fastest.
Arguments:
- state: float32 [3, 1024, 2048], P(None, 'tile', 'pole'), may hold values from -6 to 6
- depth: float32 [1024, 2048], P('tile', 'pole'), may hold values from 0.5 to 2
- pole_real: float32 [16], P('pole'), may hold values from -1.5 to -0.5
- pole_imag: float32 [16], P('pole'), may hold values from -2 to 2
- pole_weight: float32 [2, 16], P(None, 'pole'), may hold values from -3 to 3
Outputs:
- advanced: float32 [3, 1024, 2048], P(None, 'tile', 'pole')
All inputs are finite; a program needn't handle non-finite values.
Results may differ from a plain program's by a relative error of at most 0.00002.
Values sent between devices are 32-bit elements; how exact they have to be, the bound alone decides.
A program may use at most 64 MiB of HBM per device.

v0:
```python
import jax
import jax.numpy as jnp
from jax import lax
from jax.experimental import pallas as pl
from jax.experimental.pallas import tpu as pltpu
from jax.sharding import PartitionSpec as P

MESH = pl.DeviceIdType.MESH
ITERS = 8
CORIOLIS = 0.7
OWN = 16
ROWS = 3 * OWN
LANES = 128


def times(left, right):
    return (
        left[0] * right[0] - left[1] * right[1],
        left[0] * right[1] + left[1] * right[0],
    )


def inverse(value):
    norm = value[0] * value[0] + value[1] * value[1]
    return (value[0] / norm, -value[1] / norm)


def scaled(factor, value):
    return (factor * value[0], factor * value[1])


def coefficient_tile(real_ref, imag_ref, weight_ref, poles):
    lane = lax.broadcasted_iota(jnp.int32, (8, LANES), 1)
    row = lax.broadcasted_iota(jnp.int32, (8, LANES), 0)
    alpha = [jnp.full((8, LANES), -1.0, jnp.float32), jnp.zeros((8, LANES), jnp.float32)]
    beta = [jnp.zeros((8, LANES), jnp.float32)] * 2
    for k in range(poles):
        here = lane == k
        alpha[0] = jnp.where(here, real_ref[k], alpha[0])
        alpha[1] = jnp.where(here, imag_ref[k], alpha[1])
        beta[0] = jnp.where(here, weight_ref[0, k], beta[0])
        beta[1] = jnp.where(here, weight_ref[1, k], beta[1])
    square = times(alpha, alpha)
    shift = (square[0] + CORIOLIS * CORIOLIS, square[1])
    sigma = ((shift[0] + 8.0) * 0.125, shift[1] * 0.125)
    twice = scaled(2.0, sigma)
    second = [(jnp.ones_like(lane, jnp.float32), jnp.zeros_like(lane, jnp.float32)), twice]
    for _ in range(ITERS - 2):
        product = times(twice, second[-1])
        second.append((product[0] - second[-2][0], product[1] - second[-2][1]))
    product = times(sigma, second[7])
    last = (product[0] - second[6][0], product[1] - second[6][1])
    kappa = scaled(0.125, inverse(last))
    order_real, order_imag = second[7]
    for m in range(1, ITERS):
        order_real = jnp.where(row == m, 2.0 * second[7 - m][0], order_real)
        order_imag = jnp.where(row == m, 2.0 * second[7 - m][1], order_imag)
    over_alpha = inverse(alpha)
    gamma = times(beta, inverse(shift))
    gamma_alpha = times(gamma, alpha)
    weighted = times(kappa, beta)
    gammas = times(kappa, gamma)
    weighted_over = times(weighted, over_alpha)
    gammas_over = times(gammas, over_alpha)
    gammas_alpha = times(gammas, alpha)
    pieces = (
        times(weighted_over, shift),
        scaled(-1.0, weighted),
        scaled(-CORIOLIS, weighted_over),
        scaled(0.5, weighted),
        scaled(-0.5, gammas_alpha),
        scaled(-0.5 * CORIOLIS, gammas),
        scaled(0.5 * CORIOLIS, weighted_over),
        scaled(-0.5 * CORIOLIS, gammas),
        scaled(-0.5 * CORIOLIS * CORIOLIS, gammas_over),
    )
    sums = [piece[0] * order_real - piece[1] * order_imag for piece in pieces]
    sums += [gamma_alpha[0], CORIOLIS * gamma[0]]
    tile = jnp.zeros((8, LANES), jnp.float32)
    for index, value in enumerate(sums):
        tile = jnp.where(lane == index, jnp.sum(value, axis=1, keepdims=True), tile)
    return tile


def kernel(
    state_ref, depth_ref, real_ref, imag_ref, weight_ref, out_ref,
    block, edges, left_edges, right_edges, mine, theirs, table,
    real_s, imag_s, weight_s,
    flux, face, north, south, middle, chain, slope,
    load_sem, send_sem, recv_sem,
):
    poles = real_s.shape[0]
    tiles_of = state_ref.shape[2] // LANES
    p, t = lax.axis_index("pole"), lax.axis_index("tile")
    n_pole, n_tile = lax.axis_size("pole"), lax.axis_size("tile")
    peers_p = [lax.rem(p + d, n_pole) for d in range(n_pole)]
    right, left = peers_p[1], peers_p[n_pole - 1]
    down, up = lax.rem(t + 1, n_tile), lax.rem(t + n_tile - 1, n_tile)

    barrier = pltpu.get_barrier_semaphore()
    around = [(left, up), (p, up), (right, up), (left, t), (right, t), (left, down), (p, down), (right, down)]
    around += [(peers_p[d], t) for d in range(2, n_pole - 1)]
    for to in around:
        pl.semaphore_signal(barrier, inc=1, device_id=to, device_id_type=MESH)

    loads = [
        pltpu.make_async_copy(real_ref, real_s, load_sem.at[0]),
        pltpu.make_async_copy(imag_ref, imag_s, load_sem.at[1]),
        pltpu.make_async_copy(weight_ref, weight_s, load_sem.at[2]),
    ]
    for c in range(tiles_of):
        columns = pl.ds(c * LANES, LANES)
        loads.append(pltpu.make_async_copy(
            state_ref.at[:, :, columns], block.at[0:3, c, OWN:2 * OWN, :], load_sem.at[3 + 2 * c]))
        loads.append(pltpu.make_async_copy(
            depth_ref.at[:, columns], block.at[3, c, OWN:2 * OWN, :], load_sem.at[4 + 2 * c]))
    for copy in loads:
        copy.start()
    for copy in loads[3:]:
        copy.wait()

    lane = lax.broadcasted_iota(jnp.int32, (OWN, LANES), 1)
    group = ((lane + 16) // 32) % 4
    packed = jnp.zeros((OWN, LANES), jnp.float32)
    for f in range(4):
        piece = jnp.where(lane < 64, block[f, 0, OWN:2 * OWN, :], block[f, tiles_of - 1, OWN:2 * OWN, :])
        if f:
            piece = pltpu.roll(piece, 32 * f, 1)
        packed = jnp.where(group == f, piece, packed)
    edges[...] = packed

    pl.semaphore_wait(barrier, len(around))

    def remote(index, source, target, to):
        return pltpu.make_async_remote_copy(
            src_ref=source, dst_ref=target, send_sem=send_sem.at[index], recv_sem=recv_sem.at[index],
            device_id=to, device_id_type=MESH)

    own = pl.ds(0, tiles_of)
    sends = [
        remote(0, edges, left_edges.at[0:OWN, :], (right, down)),
        remote(1, edges, right_edges.at[0:OWN, :], (left, down)),
        remote(2, edges, left_edges.at[2 * OWN:ROWS, :], (right, up)),
        remote(3, edges, right_edges.at[2 * OWN:ROWS, :], (left, up)),
        remote(4, block.at[1:4, own, OWN:2 * OWN, :], block.at[1:4, own, 0:OWN, :], (p, down)),
        remote(5, block.at[1:4, own, OWN:2 * OWN, :], block.at[1:4, own, 2 * OWN:ROWS, :], (p, up)),
        remote(6, block.at[0, own, 24:32, :], block.at[0, own, 8:16, :], (p, down)),
        remote(7, block.at[0, own, 16:24, :], block.at[0, own, 32:40, :], (p, up)),
        remote(8, edges, left_edges.at[OWN:2 * OWN, :], (right, t)),
        remote(9, edges, right_edges.at[OWN:2 * OWN, :], (left, t)),
    ]
    for copy in sends:
        copy.start()

    for copy in loads[:3]:
        copy.wait()
    mine[...] = coefficient_tile(real_s, imag_s, weight_s, poles)
    totals = [
        remote(9 + d, mine, theirs.at[d - 1], (peers_p[d], t)) for d in range(1, n_pole)
    ]
    for copy in totals:
        copy.start()

    for copy in sends:
        copy.wait_recv()

    halo = tiles_of
    tiles = tiles_of + 1
    wide_lane = lax.broadcasted_iota(jnp.int32, (ROWS, LANES), 1)
    both = jnp.where(wide_lane % 32 >= 16, left_edges[...], right_edges[...])
    for f in range(4):
        block[f, halo, :, :] = pltpu.roll(both, (LANES - 32 * f) % LANES, 1)

    def eastward(pieces):
        edge = lax.broadcasted_iota(jnp.int32, pieces[0].shape, 1) == LANES - 1
        turned = [pltpu.roll(piece, LANES - 1, 1) for piece in pieces]
        return [jnp.where(edge, turned[(c + 1) % tiles], turned[c]) for c in range(tiles)]

    def westward(pieces):
        edge = lax.broadcasted_iota(jnp.int32, pieces[0].shape, 1) == 0
        turned = [pltpu.roll(piece, 1, 1) for piece in pieces]
        return [jnp.where(edge, turned[(c - 1) % tiles], turned[c]) for c in range(tiles)]

    every = range(tiles)
    for c in every:
        face[c, 0:40, :] = (block[3, c, 0:40, :] + block[3, c, 1:41, :]) * 0.125
        flux[0, c, :, :] = block[3, c, :, :] * block[1, c, :, :]
        flux[1, c, :, :] = block[3, c, :, :] * block[2, c, :, :]
        chain[0, 0, c, 8:40, :] = block[0, c, 8:40, :]
    here = [block[3, c, 8:40, :] for c in every]
    beside = eastward(here)
    to_north = [(here[c] + beside[c]) * 0.125 for c in every]
    to_south = westward(to_north)
    for c in every:
        north[c, :, :] = to_north[c]
        south[c, :, :] = to_south[c]
        middle[c, :, :] = 2.0 - (face[c, 8:40, :] + face[c, 7:39, :] + to_north[c] + to_south[c])
    for which in range(2):
        here = [flux[which, c, 8:40, :] for c in every]
        after, before = eastward(here), westward(here)
        for c in every:
            along = 0.5 * (flux[which, c, 9:41, :] - flux[which, c, 7:39, :])
            across = 0.5 * (after[c] - before[c])
            if which == 0:
                chain[0, 1, c, 8:40, :] = along
                chain[0, 2, c, 8:40, :] = -across
            else:
                chain[0, 1, c, 8:40, :] = chain[0, 1, c, 8:40, :] + across
                chain[0, 2, c, 8:40, :] = chain[0, 2, c, 8:40, :] + along

    for m in range(ITERS - 1):
        first, length = (8, 32) if m < 3 else (12, 24)
        rows = slice(first, first + length)
        for f in range(3):
            here = [chain[m, f, c, rows, :] for c in every]
            after, before = eastward(here), westward(here)
            for c in every:
                inner = slice(first - 8, first - 8 + length)
                value = (
                    middle[c, inner, :] * here[c]
                    + face[c, rows, :] * chain[m, f, c, first + 1:first + 1 + length, :]
                    + face[c, first - 1:first - 1 + length, :] * chain[m, f, c, first - 1:first - 1 + length, :]
                    + north[c, inner, :] * after[c]
                    + south[c, inner, :] * before[c]
                )
                if m == 0:
                    value = 0.5 * value
                else:
                    value = value - chain[m - 1, f, c, rows, :]
                chain[m + 1, f, c, rows, :] = value

    for copy in totals:
        copy.wait_recv()
    total = mine[...]
    for d in range(n_pole - 1):
        total = total + theirs[d]
    for index in range(11):
        table[index, :, :] = jnp.broadcast_to(total[:, index:index + 1], (8, LANES))

    for c in every:
        height = jnp.zeros((OWN, LANES), jnp.float32)
        push = jnp.zeros((24, LANES), jnp.float32)
        lift = jnp.zeros((24, LANES), jnp.float32)
        for m in range(ITERS):
            for f in range(3):
                wide = chain[m, f, c, 15:39, :]
                push = push + table[3 + f, m:m + 1, :] * wide
                lift = lift + table[6 + f, m:m + 1, :] * wide
                if c < tiles_of:
                    height = height + table[f, m:m + 1, :] * chain[m, f, c, 16:32, :]
        slope[0, c, :, :] = push
        slope[1, c, :, :] = lift
        if c < tiles_of:
            out_ref[0, :, c * LANES:(c + 1) * LANES] = height
    keep_first, keep_second = table[9, 0:1, :], table[10, 0:1, :]
    here = [slope[0, c, 1:17, :] for c in every]
    push_after, push_before = eastward(here), westward(here)
    here = [slope[1, c, 1:17, :] for c in every]
    lift_after, lift_before = eastward(here), westward(here)
    for c in range(tiles_of):
        columns = slice(c * LANES, (c + 1) * LANES)
        east, north_speed = block[1, c, OWN:2 * OWN, :], block[2, c, OWN:2 * OWN, :]
        push_along = slope[0, c, 2:18, :] - slope[0, c, 0:16, :]
        lift_along = slope[1, c, 2:18, :] - slope[1, c, 0:16, :]
        out_ref[1, :, columns] = (
            keep_first * east + keep_second * north_speed
            - push_along - (lift_after[c] - lift_before[c]))
        out_ref[2, :, columns] = (
            keep_first * north_speed - keep_second * east
            - (push_after[c] - push_before[c]) + lift_along)

    for copy in sends + totals:
        copy.wait_send()


def shards(state, depth, pole_real, pole_imag, pole_weight):
    fields, rows, columns = state.shape
    poles = pole_real.shape[0]
    tiles = columns // LANES + 1
    n_pole = lax.axis_size("pole")
    copies = 10 + n_pole - 1
    f32 = jnp.float32
    return pl.pallas_call(
        kernel,
        out_shape=jax.ShapeDtypeStruct((3, rows, columns), f32),
        in_specs=[pl.BlockSpec(memory_space=pl.ANY)] * 5,
        out_specs=pl.BlockSpec(memory_space=pltpu.VMEM),
        scratch_shapes=[
            pltpu.VMEM((4, tiles, ROWS, LANES), f32),
            pltpu.VMEM((OWN, LANES), f32),
            pltpu.VMEM((ROWS, LANES), f32),
            pltpu.VMEM((ROWS, LANES), f32),
            pltpu.VMEM((8, LANES), f32),
            pltpu.VMEM((n_pole - 1, 8, LANES), f32),
            pltpu.VMEM((11, 8, LANES), f32),
            pltpu.SMEM((poles,), f32),
            pltpu.SMEM((poles,), f32),
            pltpu.SMEM((2, poles), f32),
            pltpu.VMEM((2, tiles, ROWS, LANES), f32),
            pltpu.VMEM((tiles, ROWS, LANES), f32),
            pltpu.VMEM((tiles, 32, LANES), f32),
            pltpu.VMEM((tiles, 32, LANES), f32),
            pltpu.VMEM((tiles, 32, LANES), f32),
            pltpu.VMEM((ITERS, 3, tiles, ROWS, LANES), f32),
            pltpu.VMEM((2, tiles, 24, LANES), f32),
            pltpu.SemaphoreType.DMA((3 + 2 * (tiles - 1),)),
            pltpu.SemaphoreType.DMA((copies,)),
            pltpu.SemaphoreType.DMA((copies,)),
        ],
        compiler_params=pltpu.CompilerParams(collective_id=0, has_side_effects=True),
        name="rexi_step",
    )(state, depth, pole_real, pole_imag, pole_weight)


def solution(mesh):
    return jax.shard_map(
        shards,
        mesh=mesh,
        in_specs=(
            P(None, "tile", "pole"),
            P("tile", "pole"),
            P("pole"),
            P("pole"),
            P(None, "pole"),
        ),
        out_specs=P(None, "tile", "pole"),
        check_vma=False,
    )
```

profile of v0, /device:TPU:1, one launch (start us, length us, event | category | flops | bytes accessed | tf_op | source)
XLA Modules:
  0.0 17.6 jit_solution(16118707446767005828)
XLA Ops:
  0.0 16.0 %rexi_step.1 = f32[3,16,512]{2,1,0:T(8,128)} custom-call(f32[3,16,512]{2,1,0:T(8,128)} %state_ref.1, f32[16,512]{1,0:T(8,128)} %depth_ref.1, f32[4]{0:T(128)} %real_ref.1, f32[4]{0:T(128)} %imag_ref.1, f32[2,4]{1,0:T(2,128)} %weight_ref.1), custom_call_target="tpu_custom_call" | custom-call | tf_op jit(solution)/shard_map/rexi_step/pallas_call | solution.py:283
  16.0 1.5 %copy.7 = f32[3,16,512]{2,1,0:T(8,128)} copy(f32[3,16,512]{2,1,0:T(8,128)} %rexi_step.1) | data formatting | bytes 196608
where the time goes:
time: 17.7 us; the launch traced here: 17.6 us
  Pallas kernels  16 us (90%)
  local copies, waits for them, and re-layouts  1.54 us (9%)
    pallas_call x1, Pallas kernels, shards(): pl.pallas_call(kernel, out_shape=jax.ShapeDtypeStruct((3, rows, columns),...  16 us
    unnamed x1, local copies, waits for them, and re-layouts  1.54 us

commit v1 on v0

v1 whole, which is shorter than its diff:
```python
import jax
import jax.numpy as jnp
from jax import lax
from jax.experimental import pallas as pl
from jax.experimental.pallas import tpu as pltpu
from jax.sharding import PartitionSpec as P

MESH = pl.DeviceIdType.MESH
ITERS = 8
CORIOLIS = 0.7
OWN = 16
ROWS = 3 * OWN
LANES = 128
PLANE = 8
STEPS = ((0, 1), (1, 1), (-1, 1), (1, 0), (-1, 0), (0, -1), (1, -1), (-1, -1), (2, 0))
OPPOSITE = (5, 7, 6, 4, 3, 0, 2, 1, 8)


def times(left, right):
    return (
        left[0] * right[0] - left[1] * right[1],
        left[0] * right[1] + left[1] * right[0],
    )


def inverse(value):
    norm = value[0] * value[0] + value[1] * value[1]
    return (value[0] / norm, -value[1] / norm)


def scaled(factor, value):
    return (factor * value[0], factor * value[1])


def coefficient_tile(real_ref, imag_ref, weight_ref, poles):
    lane = lax.broadcasted_iota(jnp.int32, (8, LANES), 1)
    row = lax.broadcasted_iota(jnp.int32, (8, LANES), 0)
    alpha = [jnp.full((8, LANES), -1.0, jnp.float32), jnp.zeros((8, LANES), jnp.float32)]
    beta = [jnp.zeros((8, LANES), jnp.float32)] * 2
    for k in range(poles):
        here = lane == k
        alpha[0] = jnp.where(here, real_ref[k], alpha[0])
        alpha[1] = jnp.where(here, imag_ref[k], alpha[1])
        beta[0] = jnp.where(here, weight_ref[0, k], beta[0])
        beta[1] = jnp.where(here, weight_ref[1, k], beta[1])
    square = times(alpha, alpha)
    shift = (square[0] + CORIOLIS * CORIOLIS, square[1])
    sigma = ((shift[0] + 8.0) * 0.125, shift[1] * 0.125)
    twice = scaled(2.0, sigma)
    second = [(jnp.ones_like(lane, jnp.float32), jnp.zeros_like(lane, jnp.float32)), twice]
    for _ in range(ITERS - 2):
        product = times(twice, second[-1])
        second.append((product[0] - second[-2][0], product[1] - second[-2][1]))
    product = times(sigma, second[7])
    last = (product[0] - second[6][0], product[1] - second[6][1])
    kappa = scaled(0.125, inverse(last))
    order_real, order_imag = second[7]
    for m in range(1, ITERS):
        order_real = jnp.where(row == m, 2.0 * second[7 - m][0], order_real)
        order_imag = jnp.where(row == m, 2.0 * second[7 - m][1], order_imag)
    over_alpha = inverse(alpha)
    gamma = times(beta, inverse(shift))
    gamma_alpha = times(gamma, alpha)
    weighted = times(kappa, beta)
    gammas = times(kappa, gamma)
    weighted_over = times(weighted, over_alpha)
    gammas_over = times(gammas, over_alpha)
    gammas_alpha = times(gammas, alpha)
    pieces = (
        times(weighted_over, shift),
        scaled(-1.0, weighted),
        scaled(-CORIOLIS, weighted_over),
        scaled(0.5, weighted),
        scaled(-0.5, gammas_alpha),
        scaled(-0.5 * CORIOLIS, gammas),
        scaled(0.5 * CORIOLIS, weighted_over),
        scaled(-0.5 * CORIOLIS, gammas),
        scaled(-0.5 * CORIOLIS * CORIOLIS, gammas_over),
    )
    sums = [piece[0] * order_real - piece[1] * order_imag for piece in pieces]
    sums += [gamma_alpha[0], CORIOLIS * gamma[0]]
    tile = jnp.zeros((8, LANES), jnp.float32)
    for index, value in enumerate(sums):
        tile = jnp.where(lane == index, jnp.sum(value, axis=1, keepdims=True), tile)
    return tile


def waits_for(step, p, t, n_pole, n_tile):
    dp, dt = step
    last = t == n_tile - 1
    if dt < 0:
        return jnp.logical_or(t == 0, last)
    if dt > 0:
        return None
    return jnp.logical_and(last, {1: p != n_pole - 1, -1: p == 0, 2: p < n_pole // 2}[dp])


def heard_later(step, p, t, n_pole, n_tile):
    dp, dt = step
    last = t == n_tile - 1
    if dt > 0:
        return jnp.logical_or(last, t == n_tile - 2)
    if dt < 0:
        return None
    return jnp.logical_and(last, {1: p == n_pole - 1, -1: p != 0, 2: p >= n_pole // 2}[dp])


def kernel(
    state_ref, depth_ref, real_ref, imag_ref, weight_ref, out_ref,
    block, edges, left_edges, right_edges, mine, theirs, table,
    real_s, imag_s, weight_s,
    flux, face, north, south, middle, chain, slope,
    load_sem, send_sem, recv_sem, ready_sem,
):
    poles = real_s.shape[0]
    tiles_of = state_ref.shape[2] // LANES
    p, t = lax.axis_index("pole"), lax.axis_index("tile")
    n_pole, n_tile = lax.axis_size("pole"), lax.axis_size("tile")
    peers = [(lax.rem(p + dp + n_pole, n_pole), lax.rem(t + dt + n_tile, n_tile)) for dp, dt in STEPS]
    early = [waits_for(step, p, t, n_pole, n_tile) for step in STEPS]
    late = [heard_later(step, p, t, n_pole, n_tile) for step in STEPS]

    loads = [
        pltpu.make_async_copy(real_ref, real_s, load_sem.at[0]),
        pltpu.make_async_copy(imag_ref, imag_s, load_sem.at[1]),
        pltpu.make_async_copy(weight_ref, weight_s, load_sem.at[2]),
    ]
    for c in range(tiles_of):
        columns = pl.ds(c * LANES, LANES)
        loads.append(pltpu.make_async_copy(
            state_ref.at[:, :, columns], block.at[0:3, c, OWN:2 * OWN, :], load_sem.at[3 + 2 * c]))
        loads.append(pltpu.make_async_copy(
            depth_ref.at[:, columns], block.at[3, c, OWN:2 * OWN, :], load_sem.at[4 + 2 * c]))
    for copy in loads[3:] + loads[:3]:
        copy.start()

    barrier = pltpu.get_barrier_semaphore()
    expected = jnp.int32(len(STEPS))
    for k, to in enumerate(peers):
        if early[k] is not None:
            expected = expected - early[k].astype(jnp.int32)

        def greet(to=to):
            pl.semaphore_signal(barrier, inc=1, device_id=to, device_id_type=MESH)
        if late[k] is None:
            greet()
        else:
            pl.when(jnp.logical_not(late[k]))(greet)
    pl.semaphore_wait(barrier, expected)
    for k, to in enumerate(peers):
        if late[k] is not None:
            @pl.when(late[k])
            def answer(k=k, to=to):
                pl.semaphore_signal(ready_sem.at[OPPOSITE[k]], inc=1, device_id=to, device_id_type=MESH)

    def remote(index, source, target, to):
        return pltpu.make_async_remote_copy(
            src_ref=source, dst_ref=target, send_sem=send_sem.at[index], recv_sem=recv_sem.at[index],
            device_id=to, device_id_type=MESH)

    own = pl.ds(0, tiles_of)
    lower, upper = slice(23, 32), slice(16, 25)
    above, below = slice(7, 16), slice(32, 41)
    sends = [
        remote(0, block.at[:, own, lower, :], block.at[:, own, above, :], peers[0]),
        remote(1, edges.at[7:16, :], left_edges.at[above, :], peers[1]),
        remote(2, edges.at[7:16, :], right_edges.at[above, :], peers[2]),
        remote(3, edges, left_edges.at[OWN:2 * OWN, :], peers[3]),
        remote(4, edges, right_edges.at[OWN:2 * OWN, :], peers[4]),
        remote(5, block.at[:, own, upper, :], block.at[:, own, below, :], peers[5]),
        remote(6, edges.at[0:9, :], left_edges.at[below, :], peers[6]),
        remote(7, edges.at[0:9, :], right_edges.at[below, :], peers[7]),
    ]
    from_above, from_side, from_under = sends[0:3], sends[3:5], sends[5:8]
    from_below = from_side + from_under
    totals = [
        remote(8, mine, theirs.at[0], peers[3]),
        remote(9, mine, theirs.at[1], peers[4]),
        remote(10, mine, theirs.at[2], peers[8]),
    ]

    for copy in loads[3:]:
        copy.wait()
    lane = lax.broadcasted_iota(jnp.int32, (OWN, LANES), 1)
    group = ((lane + 16) // 32) % 4
    packed = jnp.zeros((OWN, LANES), jnp.float32)
    for f in range(4):
        piece = jnp.where(lane < 64, block[f, 0, OWN:2 * OWN, :], block[f, tiles_of - 1, OWN:2 * OWN, :])
        if f:
            piece = pltpu.roll(piece, 32 * f, 1)
        packed = jnp.where(group == f, piece, packed)
    edges[...] = packed
    for k in (1, 2, 0, 3, 4, 6, 7, 5):
        if early[k] is None:
            sends[k].start()
        else:
            pl.when(jnp.logical_not(early[k]))(sends[k].start)

    for copy in loads[:3]:
        copy.wait()
    mine[...] = coefficient_tile(real_s, imag_s, weight_s, poles)
    for k, copy in ((3, totals[0]), (4, totals[1]), (8, totals[2])):
        pl.when(jnp.logical_not(early[k]))(copy.start)

    @pl.when(t == n_tile - 1)
    def _():
        for k, copies in ((5, sends[5:6]), (6, sends[6:7]), (7, sends[7:8]),
                          (3, [sends[3], totals[0]]), (4, [sends[4], totals[1]]), (8, totals[2:])):
            def send(k=k, copies=copies):
                pl.semaphore_wait(ready_sem.at[k], 1)
                for copy in copies:
                    copy.start()
            if k in (5, 6, 7):
                send()
            else:
                pl.when(early[k])(send)

    halo = tiles_of
    tiles = tiles_of + 1
    every = range(tiles)

    def eastward(pieces):
        edge = lax.broadcasted_iota(jnp.int32, pieces[0].shape, 1) == LANES - 1
        turned = [pltpu.roll(piece, LANES - 1, 1) for piece in pieces]
        return [jnp.where(edge, turned[(c + 1) % tiles], turned[c]) for c in every]

    def westward(pieces):
        edge = lax.broadcasted_iota(jnp.int32, pieces[0].shape, 1) == 0
        turned = [pltpu.roll(piece, 1, 1) for piece in pieces]
        return [jnp.where(edge, turned[(c - 1) % tiles], turned[c]) for c in every]

    def fields(m, f, c, rows):
        return chain[m, f, c, rows, :]

    def prepare(fresh, faces, columns_of, work):
        wide_lane = lax.broadcasted_iota(jnp.int32, (fresh.stop - fresh.start, LANES), 1)
        both = jnp.where(wide_lane % 32 >= 16, left_edges[fresh, :], right_edges[fresh, :])
        for f in range(4):
            block[f, halo, fresh, :] = pltpu.roll(both, (LANES - 32 * f) % LANES, 1) if f else both
        after_rows = slice(work.start + 1, work.stop + 1)
        before_rows = slice(work.start - 1, work.stop - 1)
        for c in every:
            chain[0, 0, c, fresh, :] = block[0, c, fresh, :]
            flux[0, c, fresh, :] = block[3, c, fresh, :] * block[1, c, fresh, :]
            flux[1, c, fresh, :] = block[3, c, fresh, :] * block[2, c, fresh, :]
        for c in every:
            face[c, faces, :] = (block[3, c, faces, :] + block[3, c, faces.start + 1:faces.stop + 1, :]) * 0.125
        here = [block[3, c, columns_of, :] for c in every]
        beside = eastward(here)
        to_north = [(here[c] + beside[c]) * 0.125 for c in every]
        to_south = westward(to_north)
        for c in every:
            north[c, columns_of, :] = to_north[c]
            south[c, columns_of, :] = to_south[c]
        for c in every:
            middle[c, work, :] = 2.0 - (
                face[c, work, :] + face[c, before_rows, :] + north[c, work, :] + south[c, work, :])
        here = [flux[0, c, work, :] for c in every]
        after, before = eastward(here), westward(here)
        here = [flux[1, c, work, :] for c in every]
        after_two, before_two = eastward(here), westward(here)
        for c in every:
            along = flux[0, c, after_rows, :] - flux[0, c, before_rows, :]
            along_two = flux[1, c, after_rows, :] - flux[1, c, before_rows, :]
            chain[0, 1, c, work, :] = 0.5 * (along + (after_two[c] - before_two[c]))
            chain[0, 2, c, work, :] = 0.5 * (along_two - (after[c] - before[c]))

    def advance(m, rows):
        after_rows = slice(rows.start + 1, rows.stop + 1)
        before_rows = slice(rows.start - 1, rows.stop - 1)
        for f in range(3):
            here = [fields(m, f, c, rows) for c in every]
            after, before = eastward(here), westward(here)
            for c in every:
                value = (
                    middle[c, rows, :] * here[c]
                    + face[c, rows, :] * fields(m, f, c, after_rows)
                    + face[c, before_rows, :] * fields(m, f, c, before_rows)
                    + north[c, rows, :] * after[c]
                    + south[c, rows, :] * before[c]
                )
                if m == 0:
                    value = 0.5 * value
                else:
                    value = value - fields(m - 1, f, c, rows)
                chain[m + 1, f, c, rows, :] = value

    def combine(wide, inner):
        for c in every:
            rows = wide if c < tiles_of else inner
            height = push = lift = None
            for m in range(ITERS):
                for f in range(3):
                    value = fields(m, f, c, rows)
                    one, two = table[3 + f, m:m + 1, :] * value, table[6 + f, m:m + 1, :] * value
                    push, lift = (one, two) if push is None else (push + one, lift + two)
                    if c < tiles_of:
                        part = table[f, m:m + 1, :] * fields(m, f, c, inner)
                        height = part if height is None else height + part
            slope[0, c, rows, :] = push
            slope[1, c, rows, :] = lift
            if c < tiles_of:
                out_ref[0, inner.start - OWN:inner.stop - OWN, c * LANES:(c + 1) * LANES] = height

    def spread_totals():
        for copy in totals:
            copy.wait_recv()
        total = mine[...]
        for d in range(n_pole - 1):
            total = total + theirs[d]
        for index in range(11):
            table[index, :, :] = jnp.broadcast_to(total[:, index:index + 1], (8, LANES))

    first_of_plane = lax.rem(t, PLANE) == 0

    @pl.when(first_of_plane)
    def _():
        for copy in from_below:
            copy.wait_recv()
        prepare(slice(16, 48), slice(16, 40), slice(16, 40), slice(16, 40))
        for m in range(ITERS - 1):
            advance(m, slice(16, 40) if m < 3 else slice(20, 36))
        spread_totals()
        combine(slice(24, 40), slice(24, 32))

        @pl.when(t == 0)
        def _():
            def answered(k):
                pl.semaphore_wait(ready_sem.at[k], 1)
                sends[k].start()
            pl.when(p == n_pole - 1)(lambda: answered(6))
            pl.when(p != 0)(lambda: answered(7))
            answered(5)
            pl.when(p != n_pole - 1)(lambda: answered(6))
            pl.when(p == 0)(lambda: answered(7))
        for copy in from_above:
            copy.wait_recv()
        prepare(slice(0, 16), slice(7, 16), slice(8, 16), slice(8, 24))
        for m in range(ITERS - 1):
            advance(m, slice(8, 24))
        combine(slice(8, 24), slice(16, 24))

    @pl.when(jnp.logical_not(first_of_plane))
    def _():
        for copy in from_above + from_side:
            copy.wait_recv()
        prepare(slice(0, 32), slice(7, 31), slice(8, 32), slice(8, 32))
        for m in range(ITERS - 1):
            advance(m, slice(8, 32) if m < 3 else slice(12, 28))
        spread_totals()
        combine(slice(8, 24), slice(16, 24))
        for copy in from_under:
            copy.wait_recv()
        prepare(slice(32, 48), slice(31, 39), slice(32, 40), slice(24, 40))
        for m in range(ITERS - 1):
            advance(m, slice(24, 40))
        combine(slice(24, 40), slice(24, 32))

    rows = slice(OWN, 2 * OWN)
    keep_first, keep_second = table[9, 0:1, :], table[10, 0:1, :]
    here = [slope[0, c, rows, :] for c in every]
    push_after, push_before = eastward(here), westward(here)
    here = [slope[1, c, rows, :] for c in every]
    lift_after, lift_before = eastward(here), westward(here)
    for c in range(tiles_of):
        columns = slice(c * LANES, (c + 1) * LANES)
        east, north_speed = block[1, c, rows, :], block[2, c, rows, :]
        push_along = slope[0, c, OWN + 1:2 * OWN + 1, :] - slope[0, c, OWN - 1:2 * OWN - 1, :]
        lift_along = slope[1, c, OWN + 1:2 * OWN + 1, :] - slope[1, c, OWN - 1:2 * OWN - 1, :]
        out_ref[1, :, columns] = (
            keep_first * east + keep_second * north_speed
            - push_along - (lift_after[c] - lift_before[c]))
        out_ref[2, :, columns] = (
            keep_first * north_speed - keep_second * east
            - (push_after[c] - push_before[c]) + lift_along)

    for copy in sends + totals:
        copy.wait_send()


def shards(state, depth, pole_real, pole_imag, pole_weight):
    fields, rows, columns = state.shape
    poles = pole_real.shape[0]
    tiles = columns // LANES + 1
    n_pole = lax.axis_size("pole")
    f32 = jnp.float32
    return pl.pallas_call(
        kernel,
        out_shape=pltpu.VMEM((3, rows, columns), f32),
        in_specs=[pl.BlockSpec(memory_space=pl.ANY)] * 5,
        out_specs=pl.BlockSpec(memory_space=pltpu.VMEM),
        scratch_shapes=[
            pltpu.VMEM((4, tiles, ROWS, LANES), f32),
            pltpu.VMEM((OWN, LANES), f32),
            pltpu.VMEM((ROWS, LANES), f32),
            pltpu.VMEM((ROWS, LANES), f32),
            pltpu.VMEM((8, LANES), f32),
            pltpu.VMEM((n_pole - 1, 8, LANES), f32),
            pltpu.VMEM((11, 8, LANES), f32),
            pltpu.SMEM((poles,), f32),
            pltpu.SMEM((poles,), f32),
            pltpu.SMEM((2, poles), f32),
            pltpu.VMEM((2, tiles, ROWS, LANES), f32),
            pltpu.VMEM((tiles, ROWS, LANES), f32),
            pltpu.VMEM((tiles, ROWS, LANES), f32),
            pltpu.VMEM((tiles, ROWS, LANES), f32),
            pltpu.VMEM((tiles, ROWS, LANES), f32),
            pltpu.VMEM((ITERS, 3, tiles, ROWS, LANES), f32),
            pltpu.VMEM((2, tiles, ROWS, LANES), f32),
            pltpu.SemaphoreType.DMA((3 + 2 * (tiles - 1),)),
            pltpu.SemaphoreType.DMA((11,)),
            pltpu.SemaphoreType.DMA((11,)),
            pltpu.SemaphoreType.REGULAR((len(STEPS),)),
        ],
        compiler_params=pltpu.CompilerParams(collective_id=0, has_side_effects=True),
        name="rexi_step",
    )(state, depth, pole_real, pole_imag, pole_weight)


def solution(mesh):
    return jax.shard_map(
        shards,
        mesh=mesh,
        in_specs=(
            P(None, "tile", "pole"),
            P("tile", "pole"),
            P("pole"),
            P("pole"),
            P(None, "pole"),
        ),
        out_specs=P(None, "tile", "pole"),
        check_vma=False,
    )
```

time: 17.7 us -> 13 us (0.73)
  the two profiles are of different devices: /device:TPU:1 before, /device:TPU:8 now
where the time goes in v1:
time: 13 us; the launch traced here: 12.8 us
  Pallas kernels  12.2 us (94%)
  local copies, waits for them, and re-layouts  0.64 us (5%)
    pallas_call x1, Pallas kernels, shards(): pl.pallas_call(kernel, out_shape=pltpu.VMEM((3, rows, columns), f32), in_...  12.2 us
    unnamed x1, local copies, waits for them, and re-layouts  0.64 us

profile of v1, /device:TPU:8, one launch (start us, length us, event | category | flops | bytes accessed | tf_op | source)
XLA Modules:
  0.0 12.8 jit_solution(9749428908228867042)
XLA Ops:
  0.0 12.2 %rexi_step.1 = f32[3,16,512]{2,1,0:T(8,128)S(1)} custom-call(f32[3,16,512]{2,1,0:T(8,128)} %state_ref.1, f32[16,512]{1,0:T(8,128)} %depth_ref.1, f32[4]{0:T(128)} %real_ref.1, f32[4]{0:T(128)} %imag_ref.1, f32[2,4]{1,0:T(2,128)} %weight_ref.1), custom_call_target="tpu_custom_call" | custom-call | tf_op jit(solution)/shard_map/rexi_step/pallas_call | solution.py:387
  12.2 0.6 %copy.7 = f32[3,16,512]{2,1,0:T(8,128)} copy(f32[3,16,512]{2,1,0:T(8,128)S(1)} %rexi_step.1) | data formatting | bytes 196608

commit v2 on v1

--- a/solution.py
+++ b/solution.py
@@ -109,7 +109,7 @@
     state_ref, depth_ref, real_ref, imag_ref, weight_ref, out_ref,
     block, edges, left_edges, right_edges, mine, theirs, table,
     real_s, imag_s, weight_s,
-    flux, face, north, south, middle, chain, slope,
+    flux, face, north, south, middle, chain, slope, gain, beyond,
     load_sem, send_sem, recv_sem, ready_sem,
 ):
     poles = real_s.shape[0]
@@ -184,8 +184,9 @@
     lane = lax.broadcasted_iota(jnp.int32, (OWN, LANES), 1)
     group = ((lane + 16) // 32) % 4
     packed = jnp.zeros((OWN, LANES), jnp.float32)
-    for f in range(4):
-        piece = jnp.where(lane < 64, block[f, 0, OWN:2 * OWN, :], block[f, tiles_of - 1, OWN:2 * OWN, :])
+    ends = [
+        jnp.where(lane < 64, block[f, 0, OWN:2 * OWN, :], block[f, tiles_of - 1, OWN:2 * OWN, :]) for f in range(4)]
+    for f, piece in enumerate((ends[0], ends[3] * ends[1], ends[3] * ends[2], ends[3])):
         if f:
             piece = pltpu.roll(piece, 32 * f, 1)
         packed = jnp.where(group == f, piece, packed)
@@ -219,51 +220,74 @@
     tiles = tiles_of + 1
     every = range(tiles)
 
-    def eastward(pieces):
-        edge = lax.broadcasted_iota(jnp.int32, pieces[0].shape, 1) == LANES - 1
-        turned = [pltpu.roll(piece, LANES - 1, 1) for piece in pieces]
+    def eastward(pieces, step=1, beyond_edge=None):
+        edge = lax.broadcasted_iota(jnp.int32, pieces[0].shape, 1) >= LANES - step
+        turned = [pltpu.roll(piece, LANES - step, 1) for piece in pieces[:tiles_of]]
+        turned.append(pltpu.roll(pieces[halo], LANES - step, 1) if beyond_edge is None else beyond_edge)
         return [jnp.where(edge, turned[(c + 1) % tiles], turned[c]) for c in every]
 
-    def westward(pieces):
-        edge = lax.broadcasted_iota(jnp.int32, pieces[0].shape, 1) == 0
-        turned = [pltpu.roll(piece, 1, 1) for piece in pieces]
+    def westward(pieces, step=1, beyond_edge=None):
+        edge = lax.broadcasted_iota(jnp.int32, pieces[0].shape, 1) < step
+        turned = [pltpu.roll(piece, step, 1) for piece in pieces[:tiles_of]]
+        turned.append(pltpu.roll(pieces[halo], step, 1) if beyond_edge is None else beyond_edge)
         return [jnp.where(edge, turned[(c - 1) % tiles], turned[c]) for c in every]
 
+    def side(rows):
+        wide_lane = lax.broadcasted_iota(jnp.int32, (rows.stop - rows.start, LANES), 1)
+        return jnp.where(wide_lane % 32 >= 16, left_edges[rows, :], right_edges[rows, :])
+
+    def side_field(both, f, step=0):
+        turn = (2 * LANES - 32 * f - step) % LANES
+        return pltpu.roll(both, turn, 1) if turn else both
+
+    def around(pieces, both, f):
+        return eastward(pieces, 1, side_field(both, f, 1)), westward(pieces, 1, side_field(both, f, -1))
+
     def fields(m, f, c, rows):
-        return chain[m, f, c, rows, :]
-
-    def prepare(fresh, faces, columns_of, work):
-        wide_lane = lax.broadcasted_iota(jnp.int32, (fresh.stop - fresh.start, LANES), 1)
-        both = jnp.where(wide_lane % 32 >= 16, left_edges[fresh, :], right_edges[fresh, :])
-        for f in range(4):
-            block[f, halo, fresh, :] = pltpu.roll(both, (LANES - 32 * f) % LANES, 1) if f else both
+        start = ((m * 3 + f) * tiles + c) * ROWS
+        return chain[start + rows.start:start + rows.stop, :]
+
+    def keep(m, f, c, rows, value):
+        start = ((m * 3 + f) * tiles + c) * ROWS
+        chain[start + rows.start:start + rows.stop, :] = value
+
+    def prepare(fresh, faces, columns_of, stencil, work):
+        both = side(fresh)
+        block[0, halo, fresh, :] = both
+        block[3, halo, fresh, :] = side_field(both, 3)
+        for which in range(2):
+            flux[which, halo, fresh, :] = side_field(both, 1 + which)
+        both = side(work)
         after_rows = slice(work.start + 1, work.stop + 1)
         before_rows = slice(work.start - 1, work.stop - 1)
         for c in every:
-            chain[0, 0, c, fresh, :] = block[0, c, fresh, :]
-            flux[0, c, fresh, :] = block[3, c, fresh, :] * block[1, c, fresh, :]
-            flux[1, c, fresh, :] = block[3, c, fresh, :] * block[2, c, fresh, :]
+            keep(0, 0, c, fresh, block[0, c, fresh, :])
+            if c < tiles_of:
+                flux[0, c, fresh, :] = block[3, c, fresh, :] * block[1, c, fresh, :]
+                flux[1, c, fresh, :] = block[3, c, fresh, :] * block[2, c, fresh, :]
         for c in every:
             face[c, faces, :] = (block[3, c, faces, :] + block[3, c, faces.start + 1:faces.stop + 1, :]) * 0.125
         here = [block[3, c, columns_of, :] for c in every]
-        beside = eastward(here)
+        beside, behind = around(here, both, 3)
         to_north = [(here[c] + beside[c]) * 0.125 for c in every]
-        to_south = westward(to_north)
+        to_south = [(here[c] + behind[c]) * 0.125 for c in every]
+        next_north, next_south = eastward(to_north), westward(to_south)
         for c in every:
             north[c, columns_of, :] = to_north[c]
             south[c, columns_of, :] = to_south[c]
-        for c in every:
-            middle[c, work, :] = 2.0 - (
-                face[c, work, :] + face[c, before_rows, :] + north[c, work, :] + south[c, work, :])
-        here = [flux[0, c, work, :] for c in every]
-        after, before = eastward(here), westward(here)
-        here = [flux[1, c, work, :] for c in every]
-        after_two, before_two = eastward(here), westward(here)
+            beyond[0, c, columns_of, :] = next_north[c]
+            beyond[1, c, columns_of, :] = next_south[c]
+        for c in every:
+            middle[c, stencil, :] = 2.0 - (
+                face[c, stencil, :] + face[c, stencil.start - 1:stencil.stop - 1, :]
+                + north[c, stencil, :] + south[c, stencil, :])
+        after, before = around([flux[0, c, work, :] for c in every], both, 1)
+        after_two, before_two = around([flux[1, c, work, :] for c in every], both, 2)
         for c in every:
             along = flux[0, c, after_rows, :] - flux[0, c, before_rows, :]
             along_two = flux[1, c, after_rows, :] - flux[1, c, before_rows, :]
-            chain[0, 1, c, work, :] = 0.5 * (along + (after_two[c] - before_two[c]))
-            chain[0, 2, c, work, :] = 0.5 * (along_two - (after[c] - before[c]))
+            keep(0, 1, c, work, 0.5 * (along + (after_two[c] - before_two[c])))
+            keep(0, 2, c, work, 0.5 * (along_two - (after[c] - before[c])))
 
     def advance(m, rows):
         after_rows = slice(rows.start + 1, rows.stop + 1)
@@ -283,11 +307,54 @@
                     value = 0.5 * value
                 else:
                     value = value - fields(m - 1, f, c, rows)
-                chain[m + 1, f, c, rows, :] = value
+                keep(m + 1, f, c, rows, value)
+
+    def advance_twice(m, rows, then):
+        def beside_rows(window, by):
+            return slice(window.start + by, window.stop + by)
+
+        three = range(3)
+        up, down = beside_rows(then, 1), beside_rows(then, -1)
+        here = [[fields(m, f, c, rows) for c in every] for f in three]
+        here_two = [[fields(m, f, c, then) for c in every] for f in three]
+        after, before = [eastward(x) for x in here], [westward(x) for x in here]
+        plain = [[
+            middle[c, then, :] * here_two[f][c]
+            + face[c, then, :] * fields(m, f, c, up)
+            + face[c, down, :] * fields(m, f, c, down)
+            - fields(m - 1, f, c, then)
+            for c in every] for f in three]
+        plain_after, plain_before = [eastward(x) for x in plain], [westward(x) for x in plain]
+        after_two, before_two = [eastward(x, 2) for x in here_two], [westward(x, 2) for x in here_two]
+        for f in three:
+            for c in every:
+                keep(m + 1, f, c, rows, (
+                    middle[c, rows, :] * here[f][c]
+                    + face[c, rows, :] * fields(m, f, c, beside_rows(rows, 1))
+                    + face[c, beside_rows(rows, -1), :] * fields(m, f, c, beside_rows(rows, -1))
+                    - fields(m - 1, f, c, rows)
+                    + north[c, rows, :] * after[f][c]
+                    + south[c, rows, :] * before[f][c]
+                ))
+        for f in three:
+            for c in every:
+                to_north, to_south = north[c, then, :], south[c, then, :]
+                next_after = (
+                    plain_after[f][c] + to_north * here_two[f][c] + beyond[0, c, then, :] * after_two[f][c])
+                next_before = (
+                    plain_before[f][c] + to_south * here_two[f][c] + beyond[1, c, then, :] * before_two[f][c])
+                keep(m + 2, f, c, then, (
+                    middle[c, then, :] * fields(m + 1, f, c, then)
+                    + face[c, then, :] * fields(m + 1, f, c, up)
+                    + face[c, down, :] * fields(m + 1, f, c, down)
+                    - here_two[f][c]
+                    + to_north * next_after
+                    + to_south * next_before
+                ))
 
     def combine(wide, inner):
         for c in every:
-            rows = wide if c < tiles_of else inner
+            rows = wide
             height = push = lift = None
             for m in range(ITERS):
                 for f in range(3):
@@ -311,17 +378,50 @@
         for index in range(11):
             table[index, :, :] = jnp.broadcast_to(total[:, index:index + 1], (8, LANES))
 
+    def open_seam(seam, away, outside):
+        for c in every:
+            for which in range(2):
+                flux[which, c, outside:outside + 1, :] = jnp.zeros((1, LANES), jnp.float32)
+
+    def gains(seam, away):
+        for c in every:
+            product = None
+            gain[c, 0:1, :] = jnp.ones((1, LANES), jnp.float32)
+            for m in range(1, ITERS):
+                edge = min(seam + (m - 1) * away, seam + m * away)
+                factor = face[c, edge:edge + 1, :]
+                product = 0.5 * factor if m == 1 else product * factor
+                gain[c, m:m + 1, :] = product
+
+    def close_seam(seam, away, outside):
+        last_row = slice(seam + (ITERS - 1) * away, seam + (ITERS - 1) * away + 1)
+        for c in every:
+            parts = []
+            for which in range(2):
+                lacking = (0.5 * away) * -flux[which, c, outside:outside + 1, :]
+                part = gain[c, :, :] * lacking
+                diagonal = pl.ds(((1 + which) * tiles + c) * ROWS + seam, ITERS, stride=3 * tiles * ROWS + away)
+                chain[diagonal, :] = chain[diagonal, :] + part
+                parts.append(part[ITERS - 1:ITERS, :])
+            for potential in range(2):
+                slope[potential, c, last_row, :] = (
+                    slope[potential, c, last_row, :]
+                    + table[3 * potential + 4, ITERS - 1:ITERS, :] * parts[0]
+                    + table[3 * potential + 5, ITERS - 1:ITERS, :] * parts[1])
+
     first_of_plane = lax.rem(t, PLANE) == 0
 
     @pl.when(first_of_plane)
     def _():
         for copy in from_below:
             copy.wait_recv()
-        prepare(slice(16, 48), slice(16, 40), slice(16, 40), slice(16, 40))
+        open_seam(16, 1, 15)
+        prepare(slice(16, 48), slice(16, 40), slice(16, 40), slice(16, 40), slice(16, 40))
         for m in range(ITERS - 1):
             advance(m, slice(16, 40) if m < 3 else slice(20, 36))
+        gains(16, 1)
         spread_totals()
-        combine(slice(24, 40), slice(24, 32))
+        combine(slice(23, 39), slice(24, 32))
 
         @pl.when(t == 0)
         def _():
@@ -335,26 +435,32 @@
             pl.when(p == 0)(lambda: answered(7))
         for copy in from_above:
             copy.wait_recv()
-        prepare(slice(0, 16), slice(7, 16), slice(8, 16), slice(8, 24))
-        for m in range(ITERS - 1):
-            advance(m, slice(8, 24))
-        combine(slice(8, 24), slice(16, 24))
+        prepare(slice(0, 16), slice(8, 16), slice(8, 16), slice(9, 17), slice(8, 16))
+        close_seam(16, 1, 15)
+        advance(0, slice(9, 17))
+        for m in range(1, ITERS - 1, 2):
+            advance_twice(m, slice(9 + m, 17 + m), slice(10 + m, 18 + m))
+        combine(slice(15, 23), slice(16, 24))
 
     @pl.when(jnp.logical_not(first_of_plane))
     def _():
         for copy in from_above + from_side:
             copy.wait_recv()
-        prepare(slice(0, 32), slice(7, 31), slice(8, 32), slice(8, 32))
+        open_seam(31, -1, 32)
+        prepare(slice(0, 32), slice(7, 31), slice(8, 32), slice(8, 32), slice(8, 32))
         for m in range(ITERS - 1):
             advance(m, slice(8, 32) if m < 3 else slice(12, 28))
+        gains(31, -1)
         spread_totals()
-        combine(slice(8, 24), slice(16, 24))
+        combine(slice(9, 25), slice(16, 24))
         for copy in from_under:
             copy.wait_recv()
-        prepare(slice(32, 48), slice(31, 39), slice(32, 40), slice(24, 40))
-        for m in range(ITERS - 1):
-            advance(m, slice(24, 40))
-        combine(slice(24, 40), slice(24, 32))
+        prepare(slice(32, 48), slice(31, 39), slice(32, 40), slice(31, 39), slice(32, 40))
+        close_seam(31, -1, 32)
+        advance(0, slice(31, 39))
+        for m in range(1, ITERS - 1, 2):
+            advance_twice(m, slice(31 - m, 39 - m), slice(30 - m, 38 - m))
+        combine(slice(25, 33), slice(24, 32))
 
     rows = slice(OWN, 2 * OWN)
     keep_first, keep_second = table[9, 0:1, :], table[10, 0:1, :]
@@ -405,7 +511,9 @@
             pltpu.VMEM((tiles, ROWS, LANES), f32),
             pltpu.VMEM((tiles, ROWS, LANES), f32),
             pltpu.VMEM((tiles, ROWS, LANES), f32),
-            pltpu.VMEM((ITERS, 3, tiles, ROWS, LANES), f32),
+            pltpu.VMEM((ITERS * 3 * tiles * ROWS, LANES), f32),
+            pltpu.VMEM((2, tiles, ROWS, LANES), f32),
+            pltpu.VMEM((tiles, ITERS, LANES), f32),
             pltpu.VMEM((2, tiles, ROWS, LANES), f32),
             pltpu.SemaphoreType.DMA((3 + 2 * (tiles - 1),)),
             pltpu.SemaphoreType.DMA((11,)),

time: 13 us -> 12.8 us (0.985)
  Pallas kernels: 12.2 us -> 12 us
    pallas_call x1, Pallas kernels: 12.2 us -> 12 us  [shards(): pl.pallas_call(kernel, out_shape=pltpu.VMEM((3, rows, columns), f32), in_...]
where the time goes in v2:
time: 12.8 us; the launch traced here: 12.6 us
  Pallas kernels  12 us (94%)
  local copies, waits for them, and re-layouts  0.64 us (5%)
    pallas_call x1, Pallas kernels, shards(): pl.pallas_call(kernel, out_shape=pltpu.VMEM((3, rows, columns), f32), in_...  12 us
    unnamed x1, local copies, waits for them, and re-layouts  0.64 us

profile of v2, /device:TPU:8, one launch (start us, length us, event | category | flops | bytes accessed | tf_op | source)
XLA Modules:
  0.0 12.6 jit_solution(6611892228313904026)
XLA Ops:
  0.0 12.0 %rexi_step.1 = f32[3,16,512]{2,1,0:T(8,128)S(1)} custom-call(f32[3,16,512]{2,1,0:T(8,128)} %state_ref.1, f32[16,512]{1,0:T(8,128)} %depth_ref.1, f32[4]{0:T(128)} %real_ref.1, f32[4]{0:T(128)} %imag_ref.1, f32[2,4]{1,0:T(2,128)} %weight_ref.1), custom_call_target="tpu_custom_call" | custom-call | tf_op jit(solution)/shard_map/rexi_step/pallas_call | solution.py:493
  12.0 0.6 %copy.7 = f32[3,16,512]{2,1,0:T(8,128)} copy(f32[3,16,512]{2,1,0:T(8,128)S(1)} %rexi_step.1) | data formatting | bytes 196608

commit v3 on v2

--- a/solution.py
+++ b/solution.py
@@ -313,41 +313,37 @@
         def beside_rows(window, by):
             return slice(window.start + by, window.stop + by)
 
-        three = range(3)
-        up, down = beside_rows(then, 1), beside_rows(then, -1)
-        here = [[fields(m, f, c, rows) for c in every] for f in three]
-        here_two = [[fields(m, f, c, then) for c in every] for f in three]
-        after, before = [eastward(x) for x in here], [westward(x) for x in here]
-        plain = [[
-            middle[c, then, :] * here_two[f][c]
-            + face[c, then, :] * fields(m, f, c, up)
-            + face[c, down, :] * fields(m, f, c, down)
-            - fields(m - 1, f, c, then)
-            for c in every] for f in three]
-        plain_after, plain_before = [eastward(x) for x in plain], [westward(x) for x in plain]
-        after_two, before_two = [eastward(x, 2) for x in here_two], [westward(x, 2) for x in here_two]
-        for f in three:
+        for f in range(3):
+            here = [fields(m, f, c, rows) for c in every]
+            after, before = eastward(here), westward(here)
+            here_two = [fields(m, f, c, then) for c in every]
+            after_two, before_two = eastward(here_two, 2), westward(here_two, 2)
+            plain = [
+                middle[c, then, :] * here_two[c]
+                + face[c, then, :] * fields(m, f, c, beside_rows(then, 1))
+                + face[c, beside_rows(then, -1), :] * fields(m, f, c, beside_rows(then, -1))
+                - fields(m - 1, f, c, then)
+                for c in every
+            ]
+            plain_after, plain_before = eastward(plain), westward(plain)
             for c in every:
                 keep(m + 1, f, c, rows, (
-                    middle[c, rows, :] * here[f][c]
+                    middle[c, rows, :] * here[c]
                     + face[c, rows, :] * fields(m, f, c, beside_rows(rows, 1))
                     + face[c, beside_rows(rows, -1), :] * fields(m, f, c, beside_rows(rows, -1))
                     - fields(m - 1, f, c, rows)
-                    + north[c, rows, :] * after[f][c]
-                    + south[c, rows, :] * before[f][c]
+                    + north[c, rows, :] * after[c]
+                    + south[c, rows, :] * before[c]
                 ))
-        for f in three:
             for c in every:
                 to_north, to_south = north[c, then, :], south[c, then, :]
-                next_after = (
-                    plain_after[f][c] + to_north * here_two[f][c] + beyond[0, c, then, :] * after_two[f][c])
-                next_before = (
-                    plain_before[f][c] + to_south * here_two[f][c] + beyond[1, c, then, :] * before_two[f][c])
+                next_after = plain_after[c] + to_north * here_two[c] + beyond[0, c, then, :] * after_two[c]
+                next_before = plain_before[c] + to_south * here_two[c] + beyond[1, c, then, :] * before_two[c]
                 keep(m + 2, f, c, then, (
                     middle[c, then, :] * fields(m + 1, f, c, then)
-                    + face[c, then, :] * fields(m + 1, f, c, up)
-                    + face[c, down, :] * fields(m + 1, f, c, down)
-                    - here_two[f][c]
+                    + face[c, then, :] * fields(m + 1, f, c, beside_rows(then, 1))
+                    + face[c, beside_rows(then, -1), :] * fields(m + 1, f, c, beside_rows(then, -1))
+                    - here_two[c]
                     + to_north * next_after
                     + to_south * next_before
                 ))

time: 12.8 us -> 12.7 us (level)
  no operation moved by 1% of the time
where the time goes in v3:
time: 12.7 us; the launch traced here: 12.6 us
  Pallas kernels  12 us (94%)
  local copies, waits for them, and re-layouts  0.64 us (5%)
    pallas_call x1, Pallas kernels, shards(): pl.pallas_call(kernel, out_shape=pltpu.VMEM((3, rows, columns), f32), in_...  12 us
    unnamed x1, local copies, waits for them, and re-layouts  0.64 us

profile of v3, /device:TPU:8, one launch (start us, length us, event | category | flops | bytes accessed | tf_op | source)
XLA Modules:
  0.0 12.6 jit_solution(10321768443853651881)
XLA Ops:
  0.0 12.0 %rexi_step.1 = f32[3,16,512]{2,1,0:T(8,128)S(1)} custom-call(f32[3,16,512]{2,1,0:T(8,128)} %state_ref.1, f32[16,512]{1,0:T(8,128)} %depth_ref.1, f32[4]{0:T(128)} %real_ref.1, f32[4]{0:T(128)} %imag_ref.1, f32[2,4]{1,0:T(2,128)} %weight_ref.1), custom_call_target="tpu_custom_call" | custom-call | tf_op jit(solution)/shard_map/rexi_step/pallas_call | solution.py:489
  12.0 0.6 %copy.7 = f32[3,16,512]{2,1,0:T(8,128)} copy(f32[3,16,512]{2,1,0:T(8,128)S(1)} %rexi_step.1) | data formatting | bytes 196608
